TPU v7x, 512 devices: a 4x2x32 block of a 4x8x32 slice. The times are simulated.
512 devices in a mesh: groups: 2 (over y), seq: 32 (over z), head: 4 (over x), sub: 2 (over core).
Axes of the slice: x: 4, y: 2, z: 32, core: 2. Of those that a mesh axis runs over, the one named last changes fastest.
The devices are a block of a 4x8x32 slice.
Arguments:
- hidden: bfloat16 [8192, 7168], P(('groups', 'seq')), parts along dimension 0, may hold values from -240 to 240
- segment_ids: int32 [8192], P('groups'), parts along dimension 0, may hold values from 0 to 2, never falling along the last dimension, each value on 1 to 2048 neighbouring positions
- attn_gain: float32 [7168], replicated, may hold values from 0.1 to 1.9
- down_weight: bfloat16 [7168, 2112], P('seq', ('head', 'sub')), may hold values from -0.0625 to 0.0625
- q_gain: float32 [1536], replicated, may hold values from 0.1 to 1.9
- kv_gain: float32 [512], replicated, may hold values from 0.1 to 1.9
- q_up: bfloat16 [1536, 12288], P('seq', ('head', 'sub')), may hold values from -0.15625 to 0.15625
- key_up: bfloat16 [8192, 512], P(('head', 'sub'), 'seq'), may hold values from -8 to 8
- value_up: bfloat16 [512, 8192], P('seq', ('head', 'sub')), may hold values from -1 to 1
Outputs:
- attended: bfloat16 [8192, 8192], P(('groups', 'seq'), ('head', 'sub')), parts along dimension 0
There are 2 independent parts, one for each index of `groups`. A program takes and returns all parts, laid end to end along the dimension named above; an argument that names none is the same for every part. Nothing has to cross between parts.
Inputs may be any that keep to these rules, and one draw needn't show every extreme that they name: `segment_ids`: document numbers never fall along the pack.
All inputs are finite; a program needn't handle non-finite values.
Results may differ from a plain program's by a relative error of at most 0.014.
The roundings to bfloat16 on the way count: a program that leaves them out, or rounds other values in their place, can miss the bound.
Values may be sent and summed in bfloat16 or wider, within the bound.
A program may use at most 64 MiB of HBM per device.

v0:
```python
import functools
import math
import jax
import jax.numpy as jnp
from jax import lax
from jax.sharding import PartitionSpec as P

QL = 1536
KVL = 512
ROPE = 64
NOPE = 128
VDIM = 128
EPSILON = 1e-06
ROPE_BASE = 10000.0
LOWEST_SCORE = -1e30


def laid_out(pieces, dim):
    shape = list(pieces.shape[1:])
    shape[dim] *= pieces.shape[0]
    return jnp.moveaxis(pieces, 0, dim).reshape(shape)


def from_everyone(value, axis):
    copies = jnp.broadcast_to(value, (lax.axis_size(axis), *value.shape))
    return lax.all_to_all(copies, axis, split_axis=0, concat_axis=0, tiled=True)


def gathered_copies(value, axis, dim):
    return laid_out(from_everyone(value, axis), dim)


def rotate(values, positions):
    half_width = values.shape[-1] // 2
    frequency = ROPE_BASE ** (-jnp.arange(half_width, dtype=jnp.float32) / half_width)
    angles = positions.astype(jnp.float32)[:, None] * frequency[None, :]
    target_shape = (angles.shape[0],) + (1,) * (values.ndim - 2) + (half_width,)
    cosine = jnp.cos(angles).reshape(target_shape)
    sine_part = jnp.sin(angles).reshape(target_shape)
    leading = values[..., :half_width]
    second = values[..., half_width:]
    return jnp.concatenate(
        [leading * cosine - second * sine_part, leading * sine_part + second * cosine], axis=-1
    )


def rms_scale(values):
    return lax.rsqrt(jnp.mean(values * values, axis=-1, keepdims=True) + EPSILON)


def make_keys(columns, positions, kv_gain):
    latent_raw = columns[:, :KVL].astype(jnp.float32)
    latent = (latent_raw * rms_scale(latent_raw) * kv_gain[None, :]).astype(jnp.bfloat16)
    key_rope = rotate(columns[:, KVL:].astype(jnp.float32), positions).astype(jnp.bfloat16)
    return jnp.concatenate([latent, key_rope], axis=1)


def unchanged(carry_state):
    return carry_state


def local(hidden, segment_ids, attn_gain, down_weight, q_gain, kv_gain, q_up, key_up, value_up):
    row_count = hidden.shape[0]
    half_rows = row_count // 2
    cycle_index = lax.axis_index("seq")
    positions = cycle_index * row_count + jnp.arange(row_count, dtype=jnp.int32)
    own_segments = jnp.take(segment_ids, positions)
    widened = hidden.astype(jnp.float32)
    inverse = rms_scale(widened)
    scaled = (widened * attn_gain[None, :]).astype(jnp.bfloat16)
    chosen = scaled
    down_part = jnp.dot(
        chosen,
        lax.all_gather(down_weight, "seq", axis=0, tiled=True),
        preferred_element_type=jnp.float32,
    )
    down_part = (down_part * inverse).astype(jnp.bfloat16)
    projected = lax.all_gather(down_part, ("head", "sub"), axis=1, tiled=True)
    query_low = projected[:, :QL].astype(jnp.float32)
    query_latent = (query_low * rms_scale(query_low) * q_gain[None, :]).astype(jnp.bfloat16)
    head_count = q_up.shape[1] // (NOPE + ROPE)
    chosen = query_latent
    query_full = jnp.dot(
        chosen, lax.all_gather(q_up, "seq", axis=0, tiled=True), preferred_element_type=jnp.float32
    )
    query_full = query_full.astype(jnp.bfloat16).reshape(row_count, head_count, NOPE + ROPE)
    query_rope = rotate(query_full[:, :, NOPE:].astype(jnp.float32), positions).astype(jnp.bfloat16)
    query_nope = query_full[:, :, :NOPE]
    shard_piece = gathered_copies(key_up, "seq", 1)
    blocks = shard_piece.reshape(head_count, NOPE, shard_piece.shape[1])
    absorbed = jnp.einsum(
        "thc,hcn->thn", query_nope, blocks, preferred_element_type=jnp.float32
    ).astype(jnp.bfloat16)
    queries = jnp.concatenate([absorbed, query_rope], axis=2)
    score_scale = (NOPE + ROPE) ** (-0.5)
    halves = (queries[:half_rows], queries[half_rows:])
    half_pos = (positions[:half_rows], positions[half_rows:])
    half_seg = (own_segments[:half_rows], own_segments[half_rows:])

    def attend(carry_state, key_block, key_pos, key_seg, half_index):
        running_max, running_sum, accumulator = carry_state
        scores = (
            jnp.einsum(
                "thc,nc->htn", halves[half_index], key_block, preferred_element_type=jnp.float32
            )
            * score_scale
        )
        allowed = (key_pos[None, :] <= half_pos[half_index][:, None]) & (
            key_seg[None, :] == half_seg[half_index][:, None]
        )
        scores = jnp.where(allowed[None], scores, -jnp.inf)
        new_max = jnp.maximum(running_max, jnp.max(scores, axis=2))
        shrink = jnp.exp(running_max - new_max)
        weights = jnp.exp(scores - new_max[:, :, None])
        running_sum = running_sum * shrink + jnp.sum(weights, axis=2)
        accumulator = accumulator * shrink[:, :, None] + jnp.einsum(
            "htn,nc->htc",
            weights.astype(jnp.bfloat16),
            key_block[:, :KVL],
            preferred_element_type=jnp.float32,
        )
        return (new_max, running_sum, accumulator)

    start_state = tuple(
        (
            (
                jnp.full((head_count, half_rows), LOWEST_SCORE, jnp.float32),
                jnp.zeros((head_count, half_rows), jnp.float32),
                jnp.zeros((head_count, half_rows, KVL), jnp.float32),
            )
            for half_index in range(2)
        )
    )
    share_count = lax.axis_size(("head", "sub"))
    share_rows = row_count // share_count
    share_first = lax.axis_index(("head", "sub")) * share_rows
    own_columns = lax.dynamic_slice_in_dim(projected[:, QL:], share_first, share_rows, 0)
    own_positions = lax.dynamic_slice_in_dim(positions, share_first, share_rows, 0)
    own_keys = make_keys(own_columns, own_positions, kv_gain)
    shard_piece = gathered_copies(own_keys, "seq", 0)
    shard_total = shard_piece.shape[0] // share_rows
    stacked = shard_piece.reshape(shard_total, share_rows, shard_piece.shape[1])
    assembled = gathered_copies(stacked, ("head", "sub"), 1)
    assembled = assembled.reshape(shard_total * row_count, shard_piece.shape[1])
    piece_rows = assembled.shape[0]
    block_rows = math.gcd(piece_rows, row_count)
    blocks = assembled.reshape(piece_rows // block_rows, block_rows, assembled.shape[1])
    firsts = block_rows * jnp.arange(piece_rows // block_rows, dtype=jnp.int32)

    def visit_block(block_state, scan_item):
        key_block, block_start = scan_item
        key_pos = block_start + jnp.arange(block_rows, dtype=jnp.int32)
        key_seg = jnp.take(segment_ids, key_pos)
        updated = []
        for half_index in range(2):
            is_live = jnp.min(key_pos) <= jnp.max(half_pos[half_index])
            refresh = functools.partial(
                attend, key_block=key_block, key_pos=key_pos, key_seg=key_seg, half_index=half_index
            )
            updated.append(lax.cond(is_live, refresh, unchanged, block_state[half_index]))
        return (tuple(updated), None)

    final_state, unused = lax.scan(visit_block, start_state, (blocks, firsts))
    attended = jnp.concatenate(
        [
            (accumulator / running_sum[:, :, None]).astype(jnp.bfloat16)
            for running_max, running_sum, accumulator in final_state
        ],
        axis=1,
    )
    shard_piece = gathered_copies(value_up, "seq", 0)
    chosen = attended
    blocks = shard_piece.reshape(shard_piece.shape[0], head_count, VDIM)
    result = jnp.einsum("htn,nhv->thv", chosen, blocks, preferred_element_type=jnp.float32)
    result = result.reshape(row_count, head_count * VDIM).astype(jnp.bfloat16)
    return result


def solution(mesh):
    placed = (
        P(("groups", "seq"), None),
        P("groups"),
        P(),
        P("seq", ("head", "sub")),
        P(),
        P(),
        P("seq", ("head", "sub")),
        P(("head", "sub"), "seq"),
        P("seq", ("head", "sub")),
    )
    return jax.shard_map(
        local,
        mesh=mesh,
        in_specs=placed,
        out_specs=P(("groups", "seq"), ("head", "sub")),
        check_vma=False,
    )
```

profile of v0, /device:TPU:1952, one launch (start us, length us, event | category | flops | bytes accessed | tf_op | source)
XLA Modules:
  0.0 853.1 jit_solution(4573938176594299014)
XLA Ops:
  8.4 6.5 all-to-all-start.2
  15.7 113.6 %all-to-all-done.2 = bf16[32,1024,16]{1,2,0:T(8,128)(2,1)S(1)} async-done(((bf16[32,1024,16]{1,2,0:T(8,128)(2,1)}), bf16[32,1024,16]{1,2,0:T(8,128)(2,1)S(1)}, u32[]{:S(2)}, u32[]{:S(2)}) %all-to-all-start.2) | async-done | bytes 1048608 | tf_op jit(solution)/shard_map/all_to_all | solution.py:26
  130.4 6.3 all-to-all-start.3
  137.6 1.9 fusion.20
  139.6 142.9 %all-gather.6.cloned.1.call-done = bf16[32,224,264]{1,2,0:T(8,128)(2,1)} async-done(((bf16[1,224,264]{1,2,0:T(8,128)(2,1)}), bf16[32,224,264]{1,2,0:T(8,128)(2,1)}) %all-gather.6.cloned.1.call-update) | async-done | bytes 3784720 | tf_op jit(solution)/shard_map/all_gather | solution.py:74
  282.5 5.3 copy.70
  287.8 9.1 %reshape.234 = bf16[7168,264]{0,1:T(8,128)(2,1)} reshape(bf16[32,224,264]{1,0,2:T(8,128)(2,1)} %copy.70) | data formatting | bytes 7569408
  296.9 3.8 fusion.28
  300.7 13.6 %all_gather.10 = bf16[128,2112]{0,1:T(8,128)(2,1)S(1)} all-gather(bf16[128,264]{0,1:T(8,128)(2,1)S(1)} %fusion.28), channel_id=1, replica_groups=mesh['groups'=2,'seq'=32,'head'=4,'sub'=2] {'head','sub'}, dimensions={1}, use_global_device_ids=true | all-gather | bytes 608256 | tf_op jit(solution)/shard_map/all_gather | solution.py:78
  315.2 94.7 %all_to_all.20 = bf16[32,16,576]{2,1,0:T(8,128)(2,1)S(1)} all-to-all(bf16[32,16,576]{2,1,0:T(8,128)(2,1)S(1)} %broadcast_in_dim.41), channel_id=1, replica_groups=mesh['groups'=2,'seq'=32,'head'=4,'sub'=2] {'seq'}, dimensions={0} | all-to-all | bytes 1179648 | tf_op jit(solution)/shard_map/all_to_all | solution.py:26
  410.0 2.7 broadcast_in_dim.42
  412.7 5.2 all-to-all-start.1
  422.0 44.1 %all-gather.4.cloned.1.call-done = bf16[1536,1536]{1,0:T(8,128)(2,1)} async-done(((bf16[48,1536]{1,0:T(8,128)(2,1)}), bf16[1536,1536]{1,0:T(8,128)(2,1)}) %all-gather.4.cloned.1.call-update) | async-done | bytes 4718608 | tf_op jit(solution)/shard_map/all_gather | solution.py:84
  466.1 3.4 convolution_convert_fusion
  472.0 6.5 all-to-all-done.1
  478.5 5.6 copy.72
  484.4 359.2 %while.21 = (s32[]{:T(128)}, f32[8,64]{1,0:T(8,128)S(1)}, f32[8,64]{1,0:T(8,128)S(1)}, f32[8,64,512]{2,1,0:T(8,128)S(1)}, f32[8,64]{1,0:T(8,128)S(1)}, /*index=5...) while((s32[]{:T(128)}, f32[8,64]{1,0:T(8,128)S(1)}, ...), condition=%wide.region_15.17_spmd, body=%wide.region_5.16_spmd.sunk | while | flops 287232768 | bytes 7917033 | solution.py:163
  493.3 2.4 conditional.4
  504.6 2.4 conditional.4
  516.0 2.4 conditional.4
  527.3 2.4 conditional.4
  538.6 2.4 conditional.4
  550.0 2.4 conditional.4
  561.3 2.4 conditional.4
  572.7 2.4 conditional.4
  584.0 2.4 conditional.4
  595.4 2.4 conditional.4
  606.7 2.4 conditional.4
  618.0 2.4 conditional.4
  629.4 2.4 conditional.4
  640.7 2.4 conditional.4
  652.1 2.4 conditional.4
  663.4 2.4 conditional.4
  674.8 2.4 conditional.4
  686.1 2.4 conditional.4
  697.4 2.4 conditional.4
  708.8 2.4 conditional.4
  720.1 2.4 conditional.4
  731.5 2.4 conditional.4
  742.8 2.4 conditional.4
  754.2 2.4 conditional.4
  765.5 2.4 conditional.4
  776.8 2.4 conditional.4
  788.2 2.4 conditional.4
  799.5 2.4 conditional.4
  810.9 2.4 conditional.4
  822.2 2.4 conditional.4
  833.6 2.4 conditional.4
  (758 shorter events, 330.6 us)
Async XLA Ops:
  6.5 122.7 %copy-start.3 = (bf16[16,1024]{1,0:T(8,128)(2,1)S(1)}, bf16[16,1024]{1,0:T(8,128)(2,1)}, u32[]{:S(2)}) copy-start(bf16[16,1024]{1,0:T(8,128)(2,1)} %param.25) | copy-start | bytes 98308
  8.4 120.8 %all-to-all-start.2 = ((bf16[32,1024,16]{1,2,0:T(8,128)(2,1)}), bf16[32,1024,16]{1,2,0:T(8,128)(2,1)S(1)}, u32[]{:S(2)}, u32[]{:S(2)}) async-start(bf16[32,1024,16]{1,2,0:T(8,128)(2,1)} %broadcast_in_dim.43), calls=%async_computation.2 | async-start | bytes 2097152 | tf_op jit(solution)/shard_map/all_to_all | solution.py:26
  14.9 267.6 %all-gather.6.cloned.1.call-start = ((), (), s32[]{:S(2)}) async-start(), calls=%async_computation.5 | async-start | bytes 4460544 | tf_op jit(solution)/shard_map/all_gather | solution.py:74
  130.4 184.7 %all-to-all-start.3 = ((bf16[32,16,1024]{2,1,0:T(8,128)(2,1)}), bf16[32,16,1024]{2,1,0:T(8,128)(2,1)S(1)}, u32[]{:S(2)}, u32[]{:S(2)}) async-start(bf16[32,16,1024]{2,1,0:T(8,128)(2,1)} %broadcast_in_dim.44), calls=%async_computation.3 | async-start | bytes 2097152 | tf_op jit(solution)/shard_map/all_to_all | solution.py:26
  136.7 329.4 %all-gather.4.cloned.1.call-start = ((), (), s32[]{:S(2)}) async-start(), calls=%async_computation.4 | async-start | bytes 4866048 | tf_op jit(solution)/shard_map/all_gather | solution.py:84
  287.8 9.1 %copy-start.6 = (f32[7168]{0:T(1024)S(1)}, f32[7168]{0:T(1024)}, u32[]{:S(2)}) copy-start(f32[7168]{0:T(1024)} %param.19) | copy-start | bytes 86020
  296.9 18.1 %copy-start.5 = (f32[512]{0:T(512)S(1)}, f32[512]{0:T(512)}, u32[]{:S(2)}) copy-start(f32[512]{0:T(512)} %param.22) | copy-start | bytes 6148
  314.4 105.9 %copy-start.1 = (bf16[128,2112]{0,1:T(8,128)(2,1)}, bf16[128,2112]{0,1:T(8,128)(2,1)S(1)}, u32[]{:S(2)}) copy-start(bf16[128,2112]{0,1:T(8,128)(2,1)S(1)} %all_gather.10) | copy-start | bytes 1622020
  412.7 5.2 copy-start
  412.7 65.8 %all-to-all-start.1 = ((bf16[8,32,16,576]{3,2,1,0:T(8,128)(2,1)}), bf16[8,32,16,576]{3,2,1,0:T(8,128)(2,1)}, u32[]{:S(2)}, u32[]{:S(2)}) async-start(bf16[8,32,16,576]{3,2,1,0:T(8,128)(2,1)} %broadcast_in_dim.42), calls=%async_computation.1 | async-start | bytes 10485760 | tf_op jit(solution)/shard_map/all_to_all | solution.py:26
  417.9 48.2 %copy-start.4 = (f32[1536]{0:T(1024)S(1)}, f32[1536]{0:T(1024)}, u32[]{:S(2)}) copy-start(f32[1536]{0:T(1024)} %param.21) | copy-start | bytes 18436
  843.6 1.2 copy-start.2
Sparse Core Ops, SparseCore 0:
  17.8 264.6 all-gather.5
  284.6 181.5 all-gather.3
where the time goes:
time: 859 us; the launch traced here: 853 us
  waiting for transfers between devices  309 us (36%)
  local copies, waits for them, and re-layouts  118 us (14%)
  blocking collectives  108 us (13%)
  other arithmetic  104 us (12%)
  matrix products  97.9 us (11%)
  loops' own time  85.1 us (10%)
  starting transfers between devices  18 us (2%)
  between operations  13.8 us (2%)
    all_gather x1, waiting for transfers between devices, local(): lax.all_gather(down_weight, 'seq', axis=0, tiled=True)  143 us
    all_to_all x3, waiting for transfers between devices, from_everyone(): return lax.all_to_all(copies, axis, split_axis=0, concat_axis=0, tiled=True)  120 us
    all_to_all x1, blocking collectives, from_everyone(): return lax.all_to_all(copies, axis, split_axis=0, concat_axis=0, tiled=True)  94.7 us
    another operation x1, loops' own time, local(): final_state, unused = lax.scan(visit_block, start_state, (blocks, firsts))  81.2 us
    dot_general x62, matrix products, attend(): jnp.einsum('thc,nc->htn', halves[half_index], key_block, preferred_elemen...  59.4 us
    all_gather x1, waiting for transfers between devices, local(): lax.all_gather(q_up, 'seq', axis=0, tiled=True)  44.1 us
    reduce_min x32, other arithmetic, visit_block(): is_live = jnp.min(key_pos) <= jnp.max(half_pos[half_index])  39.4 us
    gather x32, local copies, waits for them, and re-layouts, visit_block(): key_seg = jnp.take(segment_ids, key_pos)  36.7 us
  transfers between devices with their start and end apart: 5, of which 4 were waited for; matrix products, arithmetic and copies ran while one was open for 4% of the time, Pallas kernels for 0%

commit v1 on v0

--- a/solution.py
+++ b/solution.py
@@ -81,7 +81,11 @@
     head_count = q_up.shape[1] // (NOPE + ROPE)
     chosen = query_latent
     query_full = jnp.dot(
-        chosen, lax.all_gather(q_up, "seq", axis=0, tiled=True), preferred_element_type=jnp.float32
+        chosen,
+        jnp.concatenate(
+            lax.all_to_all(jnp.stack([q_up] * lax.axis_size("seq")), "seq", 0, 0), axis=0
+        ),
+        preferred_element_type=jnp.float32,
     )
     query_full = query_full.astype(jnp.bfloat16).reshape(row_count, head_count, NOPE + ROPE)
     query_rope = rotate(query_full[:, :, NOPE:].astype(jnp.float32), positions).astype(jnp.bfloat16)

time: 859 us -> 1290 us (1.50)
  waiting for transfers between devices: 309 us -> 669 us
  blocking collectives: 108 us -> 164 us
    all_to_all x0 -> x1, waiting for transfers between devices: none -> 411 us  [local(): lax.all_to_all(jnp.stack([q_up] * lax.axis_size('seq')), 'seq', 0, 0)]
    all_to_all x1 -> x2, blocking collectives: 94.7 us -> 151 us  [from_everyone(): return lax.all_to_all(copies, axis, split_axis=0, concat_axis=0, tiled=True)]
    all_gather x1 -> x0, waiting for transfers between devices: 44.1 us -> none  [local(): lax.all_gather(q_up, 'seq', axis=0, tiled=True)]
    all_to_all x3 -> x2, waiting for transfers between devices: 120 us -> 114 us  [from_everyone(): return lax.all_to_all(copies, axis, split_axis=0, concat_axis=0, tiled=True)]
  transfers between devices with their start and end apart: 5 -> 4, of which waited for: 4 -> 3; matrix products, arithmetic and copies ran while one was open for 4% -> 2% of each run, Pallas kernels for 0% -> 0%
where the time goes in v1:
time: 1290 us
  waiting for transfers between devices  669 us (52%)
  blocking collectives  164 us (13%)
  local copies, waits for them, and re-layouts  121 us (9%)
  other arithmetic  109 us (8%)
  matrix products  97.7 us (8%)
  loops' own time  87.1 us (7%)
  starting transfers between devices  23.3 us (2%)
  between operations  13.8 us (1%)
    all_to_all x1, waiting for transfers between devices, local(): lax.all_to_all(jnp.stack([q_up] * lax.axis_size('seq')), 'seq', 0, 0)  411 us
    all_to_all x2, blocking collectives, from_everyone(): return lax.all_to_all(copies, axis, split_axis=0, concat_axis=0, tiled=True)  151 us
    all_gather x1, waiting for transfers between devices, local(): lax.all_gather(down_weight, 'seq', axis=0, tiled=True)  144 us
    all_to_all x2, waiting for transfers between devices, from_everyone(): return lax.all_to_all(copies, axis, split_axis=0, concat_axis=0, tiled=True)  114 us
    another operation x1, loops' own time, local(): final_state, unused = lax.scan(visit_block, start_state, (blocks, firsts))  83.2 us
    dot_general x62, matrix products, attend(): jnp.einsum('thc,nc->htn', halves[half_index], key_block, preferred_elemen...  59.3 us
    select_n x64, other arithmetic, visit_block(): key_seg = jnp.take(segment_ids, key_pos)  40.8 us
    reduce_min x32, other arithmetic, visit_block(): is_live = jnp.min(key_pos) <= jnp.max(half_pos[half_index])  40.6 us
  transfers between devices with their start and end apart: 4, of which 3 were waited for; matrix products, arithmetic and copies ran while one was open for 2% of the time, Pallas kernels for 0%

profile of v1, /device:TPU:1952, one launch (start us, length us, event | category | flops | bytes accessed | tf_op | source)
XLA Modules:
  0.0 1285.2 jit_solution(8249262806981224368)
XLA Ops:
  8.4 6.5 all-to-all-start.3
  15.7 113.6 %all-to-all-done.3 = bf16[32,1024,16]{1,2,0:T(8,128)(2,1)S(1)} async-done(((bf16[32,1024,16]{1,2,0:T(8,128)(2,1)}), bf16[32,1024,16]{1,2,0:T(8,128)(2,1)S(1)}, u32[]{:S(2)}, u32[]{:S(2)}) %all-to-all-start.3) | async-done | bytes 1048608 | tf_op jit(solution)/shard_map/all_to_all | solution.py:26
  130.4 6.3 all-to-all-start.4
  136.8 1.9 fusion.20
  138.8 143.6 %all-gather.3.cloned.1.call-done = bf16[32,224,264]{1,2,0:T(8,128)(2,1)} async-done(((bf16[1,224,264]{1,2,0:T(8,128)(2,1)}), bf16[32,224,264]{1,2,0:T(8,128)(2,1)}) %all-gather.3.cloned.1.call-update) | async-done | bytes 3784720 | tf_op jit(solution)/shard_map/all_gather | solution.py:74
  282.4 5.3 copy.70
  287.7 9.1 reshape.240
  296.8 3.8 fusion.28
  300.7 13.6 %all_gather.7 = bf16[128,2112]{0,1:T(8,128)(2,1)S(1)} all-gather(bf16[128,264]{0,1:T(8,128)(2,1)S(1)} %fusion.28), channel_id=1, replica_groups=mesh['groups'=2,'seq'=32,'head'=4,'sub'=2] {'head','sub'}, dimensions={1}, use_global_device_ids=true | all-gather | bytes 608256 | tf_op jit(solution)/shard_map/all_gather | solution.py:78
  315.2 86.2 %all_to_all.25 = bf16[32,16,576]{2,1,0:T(8,128)(2,1)S(1)} all-to-all(bf16[32,16,576]{2,1,0:T(8,128)(2,1)S(1)} %broadcast_in_dim.41), channel_id=1, replica_groups=mesh['groups'=2,'seq'=32,'head'=4,'sub'=2] {'seq'}, dimensions={0} | all-to-all | bytes 1179648 | tf_op jit(solution)/shard_map/all_to_all | solution.py:26
  401.8 64.6 %all_to_all.26 = bf16[8,32,16,576]{3,2,1,0:T(8,128)(2,1)} all-to-all(bf16[8,32,16,576]{3,2,1,0:T(8,128)(2,1)S(1)} %broadcast_in_dim.42), channel_id=1, replica_groups=mesh['groups'=2,'seq'=32,'head'=4,'sub'=2] {'head','sub'}, dimensions={0} | all-to-all | bytes 9437184 | tf_op jit(solution)/shard_map/all_to_all | solution.py:26
  466.4 2.6 stack.2
  469.1 10.5 all-to-all-start.2
  483.8 5.7 copy.72
  489.4 411.3 %all-to-all-done.2 = bf16[32,48,1536]{2,1,0:T(8,128)(2,1)} async-done(((bf16[32,48,1536]{2,1,0:T(8,128)(2,1)}), bf16[32,48,1536]{2,1,0:T(8,128)(2,1)}, u32[]{:S(2)}, u32[]{:S(2)}) %all-to-all-start.2) | async-done | bytes 4718624 | tf_op jit(solution)/shard_map/all_to_all | solution.py:86
  900.7 3.2 convolution_convert_fusion
  906.7 368.9 %while.21 = (s32[]{:T(128)}, f32[8,64]{1,0:T(8,128)S(1)}, f32[8,64]{1,0:T(8,128)S(1)}, f32[8,64,512]{2,1,0:T(8,128)S(1)}, f32[8,64]{1,0:T(8,128)S(1)}, /*index=5...) while((s32[]{:T(128)}, f32[8,64]{1,0:T(8,128)S(1)}, ...), condition=%wide.region_15.17_spmd, body=%wide.region_5.16_spmd.sunk | while | flops 287232768 | bytes 7917033 | solution.py:167
  916.0 2.4 conditional.4
  927.6 2.4 conditional.4
  939.3 2.4 conditional.4
  950.9 2.4 conditional.4
  962.6 2.4 conditional.4
  974.2 2.4 conditional.4
  985.8 2.4 conditional.4
  997.5 2.4 conditional.4
  1009.1 2.4 conditional.4
  1020.8 2.4 conditional.4
  1032.4 2.4 conditional.4
  1044.1 2.4 conditional.4
  1055.7 2.4 conditional.4
  1067.4 2.4 conditional.4
  1079.0 2.4 conditional.4
  1090.7 2.4 conditional.4
  1102.3 2.4 conditional.4
  1114.0 2.4 conditional.4
  1125.6 2.4 conditional.4
  1137.2 2.4 conditional.4
  1148.9 2.4 conditional.4
  1160.5 2.4 conditional.4
  1172.2 2.4 conditional.4
  1183.8 2.4 conditional.4
  1195.5 2.4 conditional.4
  1207.1 2.4 conditional.4
  1218.8 2.4 conditional.4
  1230.4 2.4 conditional.4
  1242.1 2.4 conditional.4
  1253.7 2.4 conditional.4
  1265.4 2.4 conditional.4
  (761 shorter events, 337.9 us)
Async XLA Ops:
  6.5 122.7 %copy-start.5 = (bf16[16,1024]{1,0:T(8,128)(2,1)S(1)}, bf16[16,1024]{1,0:T(8,128)(2,1)}, u32[]{:S(2)}) copy-start(bf16[16,1024]{1,0:T(8,128)(2,1)} %param.25) | copy-start | bytes 98308
  8.4 120.8 %all-to-all-start.3 = ((bf16[32,1024,16]{1,2,0:T(8,128)(2,1)}), bf16[32,1024,16]{1,2,0:T(8,128)(2,1)S(1)}, u32[]{:S(2)}, u32[]{:S(2)}) async-start(bf16[32,1024,16]{1,2,0:T(8,128)(2,1)} %broadcast_in_dim.43), calls=%async_computation.3 | async-start | bytes 2097152 | tf_op jit(solution)/shard_map/all_to_all | solution.py:26
  14.9 267.6 %all-gather.3.cloned.1.call-start = ((), (), s32[]{:S(2)}) async-start(), calls=%async_computation.5 | async-start | bytes 4460544 | tf_op jit(solution)/shard_map/all_gather | solution.py:74
  130.4 184.7 %all-to-all-start.4 = ((bf16[32,16,1024]{2,1,0:T(8,128)(2,1)}), bf16[32,16,1024]{2,1,0:T(8,128)(2,1)S(1)}, u32[]{:S(2)}, u32[]{:S(2)}) async-start(bf16[32,16,1024]{2,1,0:T(8,128)(2,1)} %broadcast_in_dim.44), calls=%async_computation.4 | async-start | bytes 2097152 | tf_op jit(solution)/shard_map/all_to_all | solution.py:26
  287.7 9.1 copy-start.8
  296.8 18.1 %copy-start.7 = (f32[512]{0:T(512)S(1)}, f32[512]{0:T(512)}, u32[]{:S(2)}) copy-start(f32[512]{0:T(512)} %param.22) | copy-start | bytes 6148
  314.3 167.7 %copy-start.1 = (bf16[128,2112]{0,1:T(8,128)(2,1)}, bf16[128,2112]{0,1:T(8,128)(2,1)S(1)}, u32[]{:S(2)}) copy-start(bf16[128,2112]{0,1:T(8,128)(2,1)S(1)} %all_gather.7) | copy-start | bytes 1622020
  401.8 64.6 %copy-start.4 = (bf16[48,1536]{1,0:T(8,128)(2,1)S(1)}, bf16[48,1536]{1,0:T(8,128)(2,1)}, u32[]{:S(2)}) copy-start(bf16[48,1536]{1,0:T(8,128)(2,1)} %param.23) | copy-start | bytes 442372
  469.1 10.6 copy-start
  469.1 431.7 %all-to-all-start.2 = ((bf16[32,48,1536]{2,1,0:T(8,128)(2,1)}), bf16[32,48,1536]{2,1,0:T(8,128)(2,1)}, u32[]{:S(2)}, u32[]{:S(2)}) async-start(bf16[32,48,1536]{2,1,0:T(8,128)(2,1)} %stack.2), calls=%async_computation.2 | async-start | bytes 9437184 | tf_op jit(solution)/shard_map/all_to_all | solution.py:86
  483.8 417.0 %copy-start.2 = (bf16[128,2112]{0,1:T(8,128)(2,1)S(1)}, bf16[128,2112]{0,1:T(8,128)(2,1)}, u32[]{:S(2)}) copy-start(bf16[128,2112]{0,1:T(8,128)(2,1)} %copy-done.1) | copy-start | bytes 1622020
  483.8 417.0 %copy-start.6 = (f32[1536]{0:T(1024)S(1)}, f32[1536]{0:T(1024)}, u32[]{:S(2)}) copy-start(f32[1536]{0:T(1024)} %param.21) | copy-start | bytes 18436
  1275.7 1.2 copy-start.3
Sparse Core Ops, SparseCore 0:
  17.8 264.5 all-gather.2
